TPU v7x, 256 devices: a whole 4x4x8 slice. The times are simulated.
256 devices in a mesh: dp: 16 (over y, x_lo, core), fsdp: 16 (over z, x_hi).
Axes of the slice: x: 4 (x_hi: 2, x_lo: 2; x = x_hi * 2 + x_lo), y: 4, z: 8, core: 2. Of those that a mesh axis runs over, the one named last changes fastest.
Arguments:
- tokens: bfloat16 [2048, 5120], P('dp'), may hold values from -6 to 6
- targets: bfloat16 [2048, 5120], P('dp'), may hold values from -12 to 12
- norm_gain: float32 [5120], replicated, may hold values from 0.5 to 1.5
- up_master: float32 [5120, 6912], P('dp', 'fsdp'), may hold values from -0.078125 to 0.078125
- down_master: float32 [6912, 5120], P('fsdp', 'dp'), may hold values from -0.078125 to 0.078125
- up_probe: int32 [160, 6912], P(None, 'fsdp'), may hold values from -2147483648 to 2147483646
- down_probe: int32 [6912, 160], P('fsdp'), may hold values from -2147483648 to 2147483646
- up_first: float32 [5120, 6912], P('dp', 'fsdp'), may hold values from -0.012 to 0.012
- up_second: float32 [5120, 6912], P('dp', 'fsdp'), may hold values from 0.0001 to 0.001
- down_first: float32 [6912, 5120], P('fsdp', 'dp'), may hold values from -0.012 to 0.012
- down_second: float32 [6912, 5120], P('fsdp', 'dp'), may hold values from 0.0001 to 0.001
Outputs:
- loss: float32 [], replicated
- up_moment: float32 [5120, 6912], P('dp', 'fsdp')
- up_curvature: float32 [5120, 6912], P('dp', 'fsdp')
- up_step: float32 [5120, 6912], P('dp', 'fsdp')
- down_moment: float32 [6912, 5120], P('fsdp', 'dp')
- down_curvature: float32 [6912, 5120], P('fsdp', 'dp')
- down_step: float32 [6912, 5120], P('fsdp', 'dp')
Inputs may be any that keep to these rules, and one draw needn't show every extreme that they name: `up_probe`: any 32-bit word; each bit gives one probe sign. `down_probe`: any 32-bit word; each bit gives one probe sign.
All inputs are finite; a program needn't handle non-finite values.
Results may differ from a plain program's by a relative error of at most 0.03.
Values may be sent and summed in bfloat16 or wider, within the bound.
No kernel may reach another device: no remote copies, remote signals or barrier semaphores. Data moves between devices by JAX's collectives and lax.ppermute only.
A program may use at most 128 MiB of HBM per device.

v0:
```python
import jax
import jax.numpy as jnp
from jax import lax
from jax.sharding import Mesh, PartitionSpec as P

BLOCK = 16
STEP = 10
N_Z = 8
norm_eps = 1e-05
beta_one = 0.9
beta_two = 0.999
adam_eps = 1e-08
DP = ("y", "xlo", "core")
FS = ("z", "xhi")


def signs_rows(probe):
    shifts = jnp.arange(32, dtype=jnp.int32)[:, None, None]
    bits = jnp.bitwise_and(jnp.right_shift(probe[None, :, :], shifts), 1)
    return (1 - 2 * bits).reshape(32 * probe.shape[0], probe.shape[1]).astype(jnp.bfloat16)


def own_signs(probe, index):
    shifts = (2 * index + jnp.arange(2, dtype=jnp.int32))[:, None, None]
    bits = jnp.bitwise_and(jnp.right_shift(probe[None, :, :], shifts), 1)
    return (1 - 2 * bits).reshape(2 * probe.shape[0], probe.shape[1]).astype(jnp.float32)


def dot_last(left, right):
    return lax.dot_general(
        left, right, (((1,), (1,)), ((), ())), preferred_element_type=jnp.float32
    )


def dot_plain(left, right):
    return jnp.dot(left, right, preferred_element_type=jnp.float32)


def dot_first(left, right):
    return lax.dot_general(
        left, right, (((0,), (0,)), ((), ())), preferred_element_type=jnp.float32
    )


def gathered(shard, axis):
    return lax.all_gather(shard, axis, axis=0, tiled=True)


def sent_to_all(shard, axis):
    devices = lax.axis_size(axis)
    return lax.all_to_all(
        jnp.broadcast_to(shard[None], (devices, *shard.shape)), axis, 0, 0, tiled=True
    )


def after(value, other):
    return lax.optimization_barrier((value, other))[0]


def interleaved(first, second):
    rows, cols = first.shape
    parts = [v.reshape(N_Z, rows // N_Z, cols) for v in (first, second)]
    return jnp.stack(parts, axis=1).reshape(2 * rows, cols)


def apart(both):
    rows, cols = both.shape
    parts = both.reshape(N_Z, 2, rows // (2 * N_Z), cols)
    return (parts[:, 0].reshape(rows // 2, cols), parts[:, 1].reshape(rows // 2, cols))


def over_pairs(value):
    total = value
    for axis, pairs in (
        ("core", ((0, 1), (1, 0))),
        ("xlo", ((0, 1), (1, 0))),
        ("y", ((0, 1), (1, 0), (2, 3), (3, 2))),
        ("y", ((0, 2), (2, 0), (1, 3), (3, 1))),
    ):
        total = total + lax.ppermute(total, axis, pairs)
    return total


def stepped(grad, diag, first, second):
    first_new = beta_one * first + (1.0 - beta_one) * grad
    second_new = beta_two * second + (1.0 - beta_two) * diag * diag
    direction = (
        first_new
        / (1.0 - beta_one**STEP)
        / (jnp.sqrt(second_new / (1.0 - beta_two**STEP)) + adam_eps)
    )
    return (first_new, second_new, direction)


def local(
    tokens,
    targets,
    norm_gain,
    up_master,
    down_master,
    up_probe,
    down_probe,
    up_first,
    up_second,
    down_first,
    down_second,
):
    rows, width = tokens.shape
    own_rows, hidden = up_master.shape
    tokens_all = jnp.float32(rows * lax.axis_size(DP))
    index = lax.axis_index(DP)
    z = lax.axis_index("z")
    up_full = gathered(up_master.astype(jnp.bfloat16), DP)
    down_own = after(down_master.T.astype(jnp.bfloat16), up_full[:16, :128])
    down_full = gathered(down_own, DP)
    up_signs = signs_rows(up_probe)
    down_probe_t = down_probe.T
    down_signs = signs_rows(down_probe_t)
    values = tokens.astype(jnp.float32)
    scale = lax.rsqrt(jnp.mean(values * values, axis=-1, keepdims=True) + norm_eps)
    normed = (values * scale * norm_gain).astype(jnp.bfloat16)
    preact_dir = dot_plain(normed, up_signs)
    preact = dot_plain(normed, up_full)
    logistic = jax.nn.sigmoid(preact)
    active = (preact * logistic).astype(jnp.bfloat16)
    slopes = logistic * (1.0 + preact * (1.0 - logistic))
    curves = logistic * (1.0 - logistic) * (2.0 + preact * (1.0 - 2.0 * logistic))
    active_dir = (slopes * preact_dir).astype(jnp.bfloat16)
    acts = interleaved(active_dir, active)
    lead = interleaved(active, active_dir)
    side = interleaved(jnp.zeros_like(active), active)
    partial = dot_last(lead, down_full) + dot_last(side, down_signs)
    partial = partial.astype(jnp.bfloat16)
    scattered = lax.psum_scatter(partial, "z", scatter_dimension=0, tiled=True)
    acts_later, normed_later = lax.optimization_barrier((acts, normed, partial))[:2]
    acts_all = sent_to_all(acts_later, DP).reshape(-1, hidden)
    inputs = lax.all_to_all(normed_later, DP, split_axis=1, concat_axis=0, tiled=True)
    other = lax.ppermute(scattered, "xhi", ((0, 1), (1, 0)))
    total = scattered.astype(jnp.float32) + other.astype(jnp.float32)
    few = rows // N_Z
    goal = lax.dynamic_slice_in_dim(targets, z * few, few, 0).astype(jnp.float32)
    less = jnp.concatenate([goal, jnp.zeros_like(goal)], axis=0)
    own_res = ((total - less) / tokens_all).astype(jnp.bfloat16)
    res_both = gathered(own_res, "z")
    res_all = lax.all_to_all(res_both, DP, split_axis=1, concat_axis=0, tiled=True)
    residual, _ = apart(res_both)
    res32 = residual.astype(jnp.float32)
    loss = over_pairs(0.5 * jnp.sum(res32 * res32) * tokens_all)
    main = dot_plain(res_both, down_full)
    extra = dot_plain(res_both, down_signs)
    grad_active, hess_active = apart(main)
    hess_active = hess_active + apart(extra)[0]
    grad_preact = (slopes * grad_active).astype(jnp.bfloat16)
    hess_preact = (curves * preact_dir * grad_active + slopes * hess_active).astype(jnp.bfloat16)
    grads_all = gathered(jnp.stack([grad_preact, hess_preact])[None], DP)
    down_hess = dot_first(res_all, acts_all)
    blocks = acts_all.shape[0] // (2 * few)
    act_all = acts_all.reshape(blocks, 2, few, hidden)[:, 1].reshape(-1, hidden)
    resid_all = res_all.reshape(blocks, 2, few, own_rows)[:, 0].reshape(-1, own_rows)
    down_grad = dot_first(resid_all, act_all)
    up_grad = dot_first(inputs, grads_all[:, 0].reshape(-1, hidden))
    up_hess = dot_first(inputs, grads_all[:, 1].reshape(-1, hidden))
    up_hut = jnp.abs(own_signs(up_probe, index) * up_hess)
    spot = lax.broadcasted_iota(jnp.int32, (hidden, hidden), 0) // BLOCK
    place = lax.broadcasted_iota(jnp.int32, (hidden, hidden), 1) // BLOCK
    average = jnp.where(spot == place, 1.0 / BLOCK, 0.0).astype(jnp.float32)
    up_diag = jnp.dot(up_hut, average, precision=lax.Precision.HIGHEST)
    down_hut = jnp.abs(own_signs(down_probe_t, index) * down_hess)
    means = jnp.mean(down_hut.reshape(own_rows // BLOCK, BLOCK, hidden), axis=1)
    down_diag = jnp.repeat(means, BLOCK, axis=0)
    up_out = stepped(up_grad, up_diag, up_first, up_second)
    down_out = stepped(down_grad, down_diag, down_first.T, down_second.T)
    return (loss, *up_out, *(v.T for v in down_out))


def solution(mesh):
    fine = Mesh(mesh.devices.reshape(4, 2, 2, N_Z, 2), (*DP, *FS))
    placed = (
        P(DP, None),
        P(DP, None),
        P(),
        P(DP, FS),
        P(FS, DP),
        P(None, FS),
        P(FS, None),
        P(DP, FS),
        P(DP, FS),
        P(FS, DP),
        P(FS, DP),
    )
    return jax.shard_map(
        local,
        mesh=fine,
        in_specs=placed,
        out_specs=(P(), P(DP, FS), P(DP, FS), P(DP, FS), P(FS, DP), P(FS, DP), P(FS, DP)),
        check_vma=False,
    )
```

profile of v0, /device:TPU:1, one launch (start us, length us, event | category | flops | bytes accessed | tf_op | source)
XLA Modules:
  0.0 328.9 jit_solution(15331444754146490073)
XLA Ops:
  7.2 2.0 convert_element_type.71
  9.2 0.0 all-gather.8.cloned.1.call-start
  9.3 1.9 convert_bitcast_fusion
  11.2 0.0 reduce-scatter.2.cloned.1.call-start
  11.2 1.8 copy.106
  13.0 0.1 shift_right_arithmetic.82
  13.1 1.9 fusion.3
  15.1 0.7 fusion.5
  15.8 4.2 %subtract_convert_fusion = bf16[32,160,432]{2,1,0:T(8,128)(2,1)} fusion(s32[160,432]{1,0:T(8,128)S(1)} %bitcast.181), kind=kLoop, calls=%fused_computation.5 | loop fusion | flops 11059200 | bytes 4700160 | tf_op jit(solution)/shard_map/convert_element_type | solution.py:20
  20.0 3.0 fusion.7
  23.0 3.3 %fusion.97 = f32[128,432]{0,1:T(8,128)S(1)} fusion(bf16[128,5120]{0,1:T(8,128)(2,1)} %fusion.7, bf16[5120,432]{1,0:T(8,128)(2,1)S(1)} %fusion.3), kind=kOutput, calls=%fused_computation.104 | convolution fusion | flops 566231040 | bytes 5955584 | tf_op jit(solution)/shard_map/dot_general | solution.py:36
  26.4 29.9 %all-gather.6.cloned.1.call-done = bf16[5120,432]{1,0:T(8,128)(2,1)} async-done(((bf16[320,432]{1,0:T(8,128)(2,1)}), bf16[5120,432]{1,0:T(8,128)(2,1)}) %all-gather.6.cloned.1.call-update) | async-done | bytes 4423696 | tf_op jit(solution)/shard_map/all_gather | solution.py:46
  56.3 4.9 %multiply_convert_fusion.3 = (bf16[128,432]{0,1:T(8,128)(2,1)S(1)}, bf16[128,432]{0,1:T(8,128)(2,1)S(1)}, f32[128,432]{0,1:T(8,128)S(1)}) fusion(f32[128,432]{0,1:T(8,128)S(1)} %fusion.97, bf16[128,5120]{0,1:T(8,128)(2,1)} %fusion.7, bf16[5120,432]{1,0:T(8,128)(2,1)} %all-gather.6.cloned.1.call-done), kind=kOutput, calls=%fused_computation.85 | convolution fusion | flops 566839296 | bytes 6397952 | tf_op jit(solution)/shard_map/dot_general | solution.py:36
  61.2 0.1 copy.107
  61.3 0.1 copy.108
  61.6 39.2 %all-gather.8.cloned.1.call-done = bf16[5120,432]{1,0:T(8,128)(2,1)} async-done(((bf16[320,432]{1,0:T(8,128)(2,1)}), bf16[5120,432]{1,0:T(8,128)(2,1)}) %all-gather.8.cloned.1.call-update) | async-done | bytes 4423696 | tf_op jit(solution)/shard_map/all_gather | solution.py:46
  100.8 4.2 %fusion.98 = f32[256,5120]{1,0:T(8,128)S(1)} fusion(bf16[256,432]{1,0:T(8,128)(2,1)S(1)} %bitcast.189, bf16[5120,432]{1,0:T(8,128)(2,1)} %all-gather.8.cloned.1.call-done), kind=kOutput, calls=%fused_computation.105 | convolution fusion | flops 1132462080 | bytes 9887744 | tf_op jit(solution)/shard_map/dot_general | solution.py:30
  105.0 3.0 fusion.4
  108.1 40.1 %reduce-scatter.2.cloned.1.call-done = bf16[32,5120]{1,0:T(8,128)(2,1)} async-done(((bf16[256,5120]{1,0:T(8,128)(2,1)}), bf16[32,5120]{1,0:T(8,128)(2,1)}) %reduce-scatter.2.cloned.1.call-update) | async-done | bytes 327696 | tf_op jit(solution)/shard_map/reduce_scatter | solution.py:134
  148.2 2.7 collective-permute-start
  150.9 4.9 %collective-permute-done = bf16[32,5120]{1,0:T(8,128)(2,1)S(1)} collective-permute-done((bf16[32,5120]{1,0:T(8,128)(2,1)}, bf16[32,5120]{1,0:T(8,128)(2,1)S(1)}, u32[]{:S(2)}, u32[]{:S(2)}) %collective-permute-start) | collective-permute-done | bytes 327712 | tf_op jit(solution)/shard_map/ppermute | solution.py:138
  155.8 1.8 multiply_convert_fusion
  157.7 0.1 copy.123
  157.9 2.0 broadcast_in_dim.15
  159.9 11.1 %all-to-all-start.2 = ((bf16[16,256,432]{1,2,0:T(8,128)(2,1)}), bf16[16,256,432]{1,2,0:T(8,128)(2,1)}, u32[]{:S(2)}, u32[]{:S(2)}) async-start(bf16[16,256,432]{1,2,0:T(8,128)(2,1)} %broadcast_in_dim.15), calls=%async_computation.3 | async-start | bytes 7077888 | tf_op jit(solution)/shard_map/all_to_all | solution.py:51
  171.0 30.5 %all-gather.10.cloned.1.call-done = bf16[256,5120]{1,0:T(8,128)(2,1)} async-done(((bf16[32,5120]{1,0:T(8,128)(2,1)}), bf16[256,5120]{1,0:T(8,128)(2,1)}) %all-gather.10.cloned.1.call-update) | async-done | bytes 2621456 | tf_op jit(solution)/shard_map/all_gather | solution.py:46
  201.5 4.8 %fusion.99 = f32[256,432]{1,0:T(8,128)S(1)} fusion(bf16[256,5120]{1,0:T(8,128)(2,1)} %all-gather.10.cloned.1.call-done, bf16[5120,432]{1,0:T(8,128)(2,1)} %all-gather.8.cloned.1.call-done), kind=kOutput, calls=%fused_computation.106 | convolution fusion | flops 1132462080 | bytes 7487488 | tf_op jit(solution)/shard_map/dot_general | solution.py:36
  206.3 0.1 copy.114
  206.5 3.8 %convolution_add_fusion.1 = f32[8,1,16,432]{3,2,1,0:T(8,128)S(1)} fusion(bf16[8,2,16,5120]{3,2,1,0:T(8,128)(2,1)} %bitcast.173, bf16[5120,432,1,1]{1,0,3,2:T(8,128)(2,1)} %bitcast.169, f32[8,2,16,432]{3,2,1,0:T(8,128)S(1)} %bitcast.193), kind=kOutput, calls=%fused_computation.34 | convolution fusion | flops 566286336 | bytes 7487488 | tf_op jit(solution)/shard_map/slice | solution.py:69
  210.2 0.1 copy.117
  210.3 0.2 fusion.87
  210.5 0.7 pad_maximum_fusion.2
  211.3 4.4 %copy.120 = bf16[256,5120]{0,1:T(8,128)(2,1)} copy(bf16[256,5120]{1,0:T(8,128)(2,1)} %all-gather.10.cloned.1.call-done) | data formatting | bytes 5242880 | tf_op jit(solution)/shard_map/all_gather | solution.py:46
  215.7 9.0 %all-to-all-start.1 = ((bf16[256,16,320]{0,2,1:T(8,128)(2,1)}), bf16[256,16,320]{0,2,1:T(8,128)(2,1)}, u32[]{:S(2)}, u32[]{:S(2)}) async-start(bf16[256,16,320]{0,2,1:T(8,128)(2,1)} %bitcast.175), calls=%async_computation.2 | async-start | bytes 5242880 | tf_op jit(solution)/shard_map/all_to_all | solution.py:145
  224.7 0.1 shift_right_arithmetic.90
  224.8 0.1 shift_right_arithmetic.91
  224.9 1.3 fusion.67
  226.2 6.1 %copy.124 = bf16[16,256,432]{2,1,0:T(8,128)(2,1)} copy(bf16[16,256,432]{1,2,0:T(8,128)(2,1)} %all-to-all-done.2) | data formatting | bytes 7077888 | tf_op jit(solution)/shard_map/all_to_all | solution.py:51
  232.3 1.8 slice.39
  234.1 3.0 copy.132
  237.1 2.6 multiply_reduce_fusion
  240.4 1.1 collective-permute-start.1
  241.5 0.1 collective-permute-done.1
  242.3 20.7 %collective-permute-start.2 = (f32[]{:T(128)}, f32[]{:T(128)}, u32[]{:S(2)}, u32[]{:S(2)}) collective-permute-start(f32[]{:T(128)} %add.106), channel_id=1, source_target_pairs={{0,32},{32,0},{1,33},{33,1},{2,34},{34,2},{3,35},{35,3},{4,36},{36... | collective-permute-start | bytes 20 | tf_op jit(solution)/shard_map/ppermute | solution.py:80
  263.0 3.6 %collective-permute-done.2 = f32[]{:T(128)} collective-permute-done((f32[]{:T(128)}, f32[]{:T(128)}, u32[]{:S(2)}, u32[]{:S(2)}) %collective-permute-start.2) | collective-permute-done | bytes 36 | tf_op jit(solution)/shard_map/ppermute | solution.py:80
  267.3 0.8 collective-permute-start.3
  268.1 2.1 collective-permute-done.3
  270.9 10.6 %collective-permute-start.4 = (f32[]{:T(128)}, f32[]{:T(128)}, u32[]{:S(2)}, u32[]{:S(2)}) collective-permute-start(f32[]{:T(128)} %add.108), channel_id=1, source_target_pairs={{0,128},{128,0},{64,192},{192,64},{1,129},{129,1},{65,193},{193,65... | collective-permute-start | bytes 20 | tf_op jit(solution)/shard_map/ppermute | solution.py:80
  281.5 0.3 collective-permute-done.4
  282.6 7.4 %all-to-all-start = ((bf16[128,16,320]{0,2,1:T(8,128)(2,1)}), bf16[128,16,320]{0,2,1:T(8,128)(2,1)}, u32[]{:S(2)}, u32[]{:S(2)}) async-start(bf16[128,16,320]{0,2,1:T(8,128)(2,1)} %bitcast.10), calls=%async_computation.1 | async-start | bytes 2621440 | tf_op jit(solution)/shard_map/all_to_all | solution.py:137
  290.0 4.5 %copy.121 = bf16[16,256,320]{2,1,0:T(8,128)(2,1)} copy(bf16[16,256,320]{1,2,0:T(8,128)(2,1)} %bitcast.21) | data formatting | bytes 5242880 | tf_op jit(solution)/shard_map/all_to_all | solution.py:145
  294.5 1.6 slice.38
  296.1 1.1 copy.131
  297.2 5.4 %fusion.25 = f32[320,432]{1,0:T(8,128)} fusion(f32[320,432]{1,0:T(8,128)} %get-tuple-element.21, bf16[16,256,432]{1,2,0:T(8,128)(2,1)} %all-to-all-done.2, bf16[256,16,320]{0,2,1:T(8,128)(2,1)} %all-to-all-done.1), kind=kOutput, calls=%fused_computation.28 | convolution fusion | flops 1132738560 | bytes 7266304 | tf_op jit(solution)/shard_map/dot_general | solution.py:40
  302.7 1.2 reduce_sum.29
  303.9 2.9 bitcast_add_fusion.1
  306.8 1.4 fusion.63
  308.2 2.2 fusion.96
  310.5 1.7 copy.129
  312.1 0.5 copy.130
  312.6 0.6 copy-done.9
  313.2 2.8 fusion.46
  316.1 2.4 fusion.41
  318.5 2.7 add_divide_fusion
  (52 shorter events, 0.5 us)
Async XLA Ops:
  7.2 143.7 %copy-start = (bf16[128,5120]{1,0:T(8,128)(2,1)S(1)}, bf16[128,5120]{1,0:T(8,128)(2,1)}, u32[]{:S(2)}) copy-start(bf16[128,5120]{1,0:T(8,128)(2,1)} %param.12) | copy-start | bytes 3932164
  7.2 5.9 %copy-start.4 = (s32[160,432]{1,0:T(8,128)S(1)}, s32[160,432]{1,0:T(8,128)}, u32[]{:S(2)}) copy-start(s32[160,432]{1,0:T(8,128)} %param.16) | copy-start | bytes 829444
  7.2 49.1 %all-gather.6.cloned.1.call-start = ((), (), s32[]{:S(2)}) async-start(), calls=%async_computation.4 | async-start | bytes 5570560 | tf_op jit(solution)/shard_map/all_gather | solution.py:46
  9.2 91.5 %all-gather.8.cloned.1.call-start = ((), (), s32[]{:S(2)}) async-start(), calls=%async_computation.5 | async-start | bytes 5570560 | tf_op jit(solution)/shard_map/all_gather | solution.py:46
  11.2 137.0 %reduce-scatter.2.cloned.1.call-start = ((), (), s32[]{:S(2)}) async-start(), calls=%async_computation.6 | async-start | bytes 2949120 | tf_op jit(solution)/shard_map/reduce_scatter | solution.py:134
  13.1 2.7 copy-start.5
  15.8 4.2 %copy-start.8 = (f32[5120]{0:T(1024)S(1)}, f32[5120]{0:T(1024)}, u32[]{:S(2)}) copy-start(f32[5120]{0:T(1024)} %param.13) | copy-start | bytes 61444
  100.8 4.2 %slice-start = ((s8[5242880]{0:T(1024)(128)(4,1)}), s8[4194304]{0:T(1024)(128)(4,1)S(1)}, s32[]{:S(2)}) async-start(s8[5242880]{0:T(1024)(128)(4,1)} %bitcast.170), calls=%async_computation.9 | async-start | bytes 8388608
  100.8 4.2 %slice-start.1 = ((s8[5242880]{0:T(1024)(128)(4,1)}), s8[1048576]{0:T(1024)(128)(4,1)S(1)}, s32[]{:S(2)}) async-start(s8[5242880]{0:T(1024)(128)(4,1)} %bitcast.170), calls=%async_computation.10 | async-start | bytes 2097152
  108.0 93.5 %all-gather.10.cloned.1.call-start = ((), (), s32[]{:S(2)}) async-start(), calls=%async_computation.7 | async-start | bytes 2949120 | tf_op jit(solution)/shard_map/all_gather | solution.py:46
  148.2 7.6 %collective-permute-start = (bf16[32,5120]{1,0:T(8,128)(2,1)}, bf16[32,5120]{1,0:T(8,128)(2,1)S(1)}, u32[]{:S(2)}, u32[]{:S(2)}) collective-permute-start(bf16[32,5120]{1,0:T(8,128)(2,1)} %reduce-scatter.2.cloned.1.call-done), channel_id=1, source_target_pairs={{0,1},{1,0},{2,3},{3,2},{4,5},{5,4},{6,7},{7,6},{8,9},{9,8},{10,11... | collective-permute-start | bytes 983048 | tf_op jit(solution)/shard_map/ppermute | solution.py:138
  159.9 55.8 %all-to-all-start.2 = ((bf16[16,256,432]{1,2,0:T(8,128)(2,1)}), bf16[16,256,432]{1,2,0:T(8,128)(2,1)}, u32[]{:S(2)}, u32[]{:S(2)}) async-start(bf16[16,256,432]{1,2,0:T(8,128)(2,1)} %broadcast_in_dim.15), calls=%async_computation.3 | async-start | bytes 7077888 | tf_op jit(solution)/shard_map/all_to_all | solution.py:51
  171.0 137.2 %all-gather.12.cloned.1.call-start = ((), (), s32[]{:S(2)}) async-start(), calls=%async_computation.8 | async-start | bytes 3760128 | tf_op jit(solution)/shard_map/all_gather | solution.py:46
  215.7 66.9 %all-to-all-start.1 = ((bf16[256,16,320]{0,2,1:T(8,128)(2,1)}), bf16[256,16,320]{0,2,1:T(8,128)(2,1)}, u32[]{:S(2)}, u32[]{:S(2)}) async-start(bf16[256,16,320]{0,2,1:T(8,128)(2,1)} %bitcast.175), calls=%async_computation.2 | async-start | bytes 5242880 | tf_op jit(solution)/shard_map/all_to_all | solution.py:145
  240.4 1.2 collective-permute-start.1
  242.3 24.3 %collective-permute-start.2 = (f32[]{:T(128)}, f32[]{:T(128)}, u32[]{:S(2)}, u32[]{:S(2)}) collective-permute-start(f32[]{:T(128)} %add.106), channel_id=1, source_target_pairs={{0,32},{32,0},{1,33},{33,1},{2,34},{34,2},{3,35},{35,3},{4,36},{36... | collective-permute-start | bytes 20 | tf_op jit(solution)/shard_map/ppermute | solution.py:80
  267.3 2.9 collective-permute-start.3
  270.9 10.9 %collective-permute-start.4 = (f32[]{:T(128)}, f32[]{:T(128)}, u32[]{:S(2)}, u32[]{:S(2)}) collective-permute-start(f32[]{:T(128)} %add.108), channel_id=1, source_target_pairs={{0,128},{128,0},{64,192},{192,64},{1,129},{129,1},{65,193},{193,65... | collective-permute-start | bytes 20 | tf_op jit(solution)/shard_map/ppermute | solution.py:80
  282.6 30.0 %all-to-all-start = ((bf16[128,16,320]{0,2,1:T(8,128)(2,1)}), bf16[128,16,320]{0,2,1:T(8,128)(2,1)}, u32[]{:S(2)}, u32[]{:S(2)}) async-start(bf16[128,16,320]{0,2,1:T(8,128)(2,1)} %bitcast.10), calls=%async_computation.1 | async-start | bytes 2621440 | tf_op jit(solution)/shard_map/all_to_all | solution.py:137
  297.2 6.7 %copy-start.2 = (bf16[128,1,16,432]{0,3,2,1:T(8,128)(2,1)S(1)}, bf16[128,1,16,432]{0,3,2,1:T(8,128)(2,1)}, u32[]{:S(2)}) copy-start(bf16[128,1,16,432]{0,3,2,1:T(8,128)(2,1)} %copy.132) | copy-start | bytes 5308420
  303.9 2.9 copy-start.3
  303.9 2.9 copy-start.6
  312.1 1.1 copy-start.9
  313.2 2.8 copy-start.7
  316.0 2.5 copy-start.11
  316.1 2.5 copy-start.10
  318.5 2.8 copy-start.1
Sparse Core Ops, SparseCore 0:
  10.4 45.8 all-gather.5
  58.7 41.9 all-gather.7
  108.2 39.9 reduce-scatter.1
  157.8 43.6 all-gather.9
  211.4 67.6 all-gather.11
where the time goes:
time: 330 us; the launch traced here: 329 us
  waiting for transfers between devices  151 us (46%)
  starting transfers between devices  63.7 us (19%)
  matrix products  40.3 us (12%)
  local copies, waits for them, and re-layouts  32.3 us (10%)
  other arithmetic  23 us (7%)
  between operations  18.7 us (6%)
    all_gather x4, waiting for transfers between devices, gathered(): return lax.all_gather(shard, axis, axis=0, tiled=True)  99.6 us
    reduce_scatter x1, waiting for transfers between devices, local(): scattered = lax.psum_scatter(partial, 'z', scatter_dimension=0, tiled=True)  40.1 us
    ppermute x4, starting transfers between devices, over_pairs(): total = total + lax.ppermute(total, axis, pairs)  33.2 us
    dot_general x4, matrix products, dot_first(): lax.dot_general(left, right, (((0,), (0,)), ((), ())), preferred_element_...  13.5 us
    dot_general x3, matrix products, dot_plain(): return jnp.dot(left, right, preferred_element_type=jnp.float32)  13.1 us
    all_to_all x1, starting transfers between devices, sent_to_all(): lax.all_to_all(jnp.broadcast_to(shard[None], (devices, *shard.shape)), ax...  11.1 us
    all_to_all x1, starting transfers between devices, local(): lax.all_to_all(res_both, DP, split_axis=1, concat_axis=0, tiled=True)  9.05 us
    unnamed x33, local copies, waits for them, and re-layouts  8.69 us
  transfers between devices with their start and end apart: 13, of which 9 were waited for; matrix products, arithmetic and copies ran while one was open for 23% of the time, Pallas kernels for 0%

commit v1 on v0

--- a/solution.py
+++ b/solution.py
@@ -43,7 +43,9 @@
 
 
 def gathered(shard, axis):
-    return lax.all_gather(shard, axis, axis=0, tiled=True)
+    return jnp.concatenate(
+        lax.all_to_all(jnp.stack([shard] * lax.axis_size(axis)), axis, 0, 0), axis=0
+    )
 
 
 def sent_to_all(shard, axis):

time: 330 us -> 472 us (1.43)
  waiting for transfers between devices: 151 us -> 265 us
  local copies, waits for them, and re-layouts: 32.3 us -> 47.8 us
  starting transfers between devices: 63.7 us -> 78.7 us
    all_to_all x0 -> x4, waiting for transfers between devices: none -> 157 us  [gathered(): lax.all_to_all(jnp.stack([shard] * lax.axis_size(axis)), axis, 0, 0)]
    all_gather x4 -> x0, waiting for transfers between devices: 99.6 us -> none  [gathered(): return lax.all_gather(shard, axis, axis=0, tiled=True)]
    all_to_all x1, waiting for transfers between devices: 0.01 us -> 31.7 us  [sent_to_all(): lax.all_to_all(jnp.broadcast_to(shard[None], (devices, *shard.shape)), ax...]
    all_to_all x1, waiting for transfers between devices: 0.01 us -> 23.7 us  [local(): lax.all_to_all(res_both, DP, split_axis=1, concat_axis=0, tiled=True)]
    all_to_all x0 -> x4, starting transfers between devices: none -> 22.7 us  [gathered(): lax.all_to_all(jnp.stack([shard] * lax.axis_size(axis)), axis, 0, 0)]
    all_to_all x1 -> x3, local copies, waits for them, and re-layouts: 4.54 us -> 15.4 us  [local(): lax.all_to_all(res_both, DP, split_axis=1, concat_axis=0, tiled=True)]
    another operation x0 -> x4, local copies, waits for them, and re-layouts: none -> 9.71 us  [gathered(): jnp.stack([shard] * lax.axis_size(axis))]
    ppermute x4, starting transfers between devices: 33.2 us -> 27.6 us  [over_pairs(): total = total + lax.ppermute(total, axis, pairs)]
  transfers between devices with their start and end apart: 13 -> 13, of which waited for: 9 -> 12; matrix products, arithmetic and copies ran while one was open for 23% -> 15% of each run, Pallas kernels for 0% -> 0%
where the time goes in v1:
time: 472 us; the launch traced here: 470 us
  waiting for transfers between devices  265 us (56%)
  starting transfers between devices  78.7 us (17%)
  local copies, waits for them, and re-layouts  47.8 us (10%)
  matrix products  40.4 us (9%)
  other arithmetic  19.1 us (4%)
  between operations  18.7 us (4%)
    all_to_all x4, waiting for transfers between devices, gathered(): lax.all_to_all(jnp.stack([shard] * lax.axis_size(axis)), axis, 0, 0)  157 us
    reduce_scatter x1, waiting for transfers between devices, local(): scattered = lax.psum_scatter(partial, 'z', scatter_dimension=0, tiled=True)  40.7 us
    all_to_all x1, waiting for transfers between devices, sent_to_all(): lax.all_to_all(jnp.broadcast_to(shard[None], (devices, *shard.shape)), ax...  31.7 us
    ppermute x4, starting transfers between devices, over_pairs(): total = total + lax.ppermute(total, axis, pairs)  27.6 us
    all_to_all x1, waiting for transfers between devices, local(): lax.all_to_all(res_both, DP, split_axis=1, concat_axis=0, tiled=True)  23.7 us
    all_to_all x4, starting transfers between devices, gathered(): lax.all_to_all(jnp.stack([shard] * lax.axis_size(axis)), axis, 0, 0)  22.7 us
    all_to_all x3, local copies, waits for them, and re-layouts, local(): lax.all_to_all(res_both, DP, split_axis=1, concat_axis=0, tiled=True)  15.4 us
    dot_general x4, matrix products, dot_first(): lax.dot_general(left, right, (((0,), (0,)), ((), ())), preferred_element_...  13.5 us
  transfers between devices with their start and end apart: 13, of which 12 were waited for; matrix products, arithmetic and copies ran while one was open for 15% of the time, Pallas kernels for 0%

profile of v1, /device:TPU:1, one launch (start us, length us, event | category | flops | bytes accessed | tf_op | source)
XLA Modules:
  0.0 470.1 jit_solution(6569844224370361344)
XLA Ops:
  7.2 1.2 convert_element_type.71
  8.4 2.8 stack.20
  11.3 7.7 %all-to-all-start = ((bf16[16,320,432]{2,1,0:T(8,128)(2,1)}), bf16[16,320,432]{2,1,0:T(8,128)(2,1)}, u32[]{:S(2)}, u32[]{:S(2)}) async-start(bf16[16,320,432]{2,1,0:T(8,128)(2,1)} %stack.20), calls=%async_computation | async-start | bytes 10485760 | tf_op jit(solution)/shard_map/all_to_all | solution.py:47
  19.0 60.8 %all-to-all-done = bf16[16,320,432]{2,1,0:T(8,128)(2,1)} async-done(((bf16[16,320,432]{2,1,0:T(8,128)(2,1)}), bf16[16,320,432]{2,1,0:T(8,128)(2,1)}, u32[]{:S(2)}, u32[]{:S(2)}) %all-to-all-start) | async-done | bytes 4423712 | tf_op jit(solution)/shard_map/all_to_all | solution.py:47
  79.8 2.8 stack.22
  82.6 5.3 %all-to-all-start.1 = ((bf16[16,320,432]{2,1,0:T(8,128)(2,1)}), bf16[16,320,432]{2,1,0:T(8,128)(2,1)}, u32[]{:S(2)}, u32[]{:S(2)}) async-start(bf16[16,320,432]{2,1,0:T(8,128)(2,1)} %stack.22), calls=%async_computation.1 | async-start | bytes 10485760 | tf_op jit(solution)/shard_map/all_to_all | solution.py:47
  87.9 1.8 copy.124
  89.8 1.9 fusion.3
  91.8 0.7 fusion.5
  92.5 4.2 subtract_convert_fusion
  96.7 3.0 fusion.7
  99.7 3.3 fusion.97
  103.1 4.9 %multiply_convert_fusion.3 = (bf16[128,432]{0,1:T(8,128)(2,1)S(1)}, bf16[128,432]{0,1:T(8,128)(2,1)S(1)}, f32[128,432]{0,1:T(8,128)S(1)}) fusion(f32[128,432]{0,1:T(8,128)S(1)} %fusion.97, bf16[128,5120]{0,1:T(8,128)(2,1)} %fusion.7, bf16[5120,432]{1,0:T(8,128)(2,1)} %bitcast), kind=kOutput, calls=%fused_computation.85 | convolution fusion | flops 566839296 | bytes 6397952 | tf_op jit(solution)/shard_map/dot_general | solution.py:36
  108.3 40.4 %all-to-all-done.1 = bf16[16,320,432]{2,1,0:T(8,128)(2,1)} async-done(((bf16[16,320,432]{2,1,0:T(8,128)(2,1)}), bf16[16,320,432]{2,1,0:T(8,128)(2,1)}, u32[]{:S(2)}, u32[]{:S(2)}) %all-to-all-start.1) | async-done | bytes 4423712 | tf_op jit(solution)/shard_map/all_to_all | solution.py:47
  148.7 4.2 fusion.98
  152.9 3.1 fusion.4
  156.1 40.7 %reduce-scatter.2.cloned.1.call-done = bf16[32,5120]{1,0:T(8,128)(2,1)} async-done(((bf16[256,5120]{1,0:T(8,128)(2,1)}), bf16[32,5120]{1,0:T(8,128)(2,1)}) %reduce-scatter.2.cloned.1.call-update) | async-done | bytes 327696 | tf_op jit(solution)/shard_map/reduce_scatter | solution.py:136
  196.8 2.7 collective-permute-start
  199.5 4.9 %collective-permute-done = bf16[32,5120]{1,0:T(8,128)(2,1)S(1)} collective-permute-done((bf16[32,5120]{1,0:T(8,128)(2,1)}, bf16[32,5120]{1,0:T(8,128)(2,1)S(1)}, u32[]{:S(2)}, u32[]{:S(2)}) %collective-permute-start) | collective-permute-done | bytes 327712 | tf_op jit(solution)/shard_map/ppermute | solution.py:140
  204.4 1.1 multiply_convert_fusion
  205.5 1.9 stack.24
  207.4 4.6 all-to-all-start.2
  212.0 0.1 copy.141
  212.2 56.1 %all-to-all-done.2 = bf16[8,32,5120]{2,1,0:T(8,128)(2,1)} async-done(((bf16[8,32,5120]{2,1,0:T(8,128)(2,1)}), bf16[8,32,5120]{2,1,0:T(8,128)(2,1)}, u32[]{:S(2)}, u32[]{:S(2)}) %all-to-all-start.2) | async-done | bytes 2621472 | tf_op jit(solution)/shard_map/all_to_all | solution.py:47
  268.3 2.0 broadcast_in_dim.12
  270.3 12.6 %all-to-all-start.6 = ((bf16[16,256,432]{1,2,0:T(8,128)(2,1)}), bf16[16,256,432]{1,2,0:T(8,128)(2,1)}, u32[]{:S(2)}, u32[]{:S(2)}) async-start(bf16[16,256,432]{1,2,0:T(8,128)(2,1)} %broadcast_in_dim.12), calls=%async_computation.7 | async-start | bytes 7077888 | tf_op jit(solution)/shard_map/all_to_all | solution.py:53
  282.9 6.0 %all_to_all.49 = bf16[256,16,320]{2,1,0:T(8,128)(2,1)} reshape(bf16[8,32,5120]{2,1,0:T(8,128)(2,1)} %all-to-all-done.2) | data formatting | bytes 5242880 | tf_op jit(solution)/shard_map/all_to_all | solution.py:147
  288.8 4.9 %copy.138 = bf16[256,16,320]{0,2,1:T(8,128)(2,1)} copy(bf16[256,16,320]{2,1,0:T(8,128)(2,1)} %all_to_all.49) | data formatting | bytes 5242880 | tf_op jit(solution)/shard_map/all_to_all | solution.py:147
  293.7 31.7 %all-to-all-done.6 = bf16[16,256,432]{1,2,0:T(8,128)(2,1)} async-done(((bf16[16,256,432]{1,2,0:T(8,128)(2,1)}), bf16[16,256,432]{1,2,0:T(8,128)(2,1)}, u32[]{:S(2)}, u32[]{:S(2)}) %all-to-all-start.6) | async-done | bytes 3538976 | tf_op jit(solution)/shard_map/all_to_all | solution.py:53
  325.4 5.2 %all-to-all-start.5 = ((bf16[256,16,320]{0,2,1:T(8,128)(2,1)}), bf16[256,16,320]{0,2,1:T(8,128)(2,1)}, u32[]{:S(2)}, u32[]{:S(2)}) async-start(bf16[256,16,320]{0,2,1:T(8,128)(2,1)} %copy.138), calls=%async_computation.6 | async-start | bytes 5242880 | tf_op jit(solution)/shard_map/all_to_all | solution.py:147
  330.5 4.8 %fusion.99 = f32[8,2,16,432]{3,2,1,0:T(8,128)S(1)} fusion(bf16[8,2,16,5120]{3,2,1,0:T(8,128)(2,1)} %bitcast.10, bf16[5120,432,1,1]{1,0,3,2:T(8,128)(2,1)} %bitcast.42), kind=kOutput, calls=%fused_computation.106 | convolution fusion | flops 1132462080 | bytes 7487488 | tf_op jit(solution)/shard_map/dot_general | solution.py:36
  335.4 0.1 copy.132
  335.5 3.8 convolution_add_fusion.1
  339.4 0.2 fusion.87
  339.6 23.7 %all-to-all-done.5 = bf16[256,16,320]{0,2,1:T(8,128)(2,1)} async-done(((bf16[256,16,320]{0,2,1:T(8,128)(2,1)}), bf16[256,16,320]{0,2,1:T(8,128)(2,1)}, u32[]{:S(2)}, u32[]{:S(2)}) %all-to-all-start.5) | async-done | bytes 2621472 | tf_op jit(solution)/shard_map/all_to_all | solution.py:147
  363.3 2.2 stack.29
  365.5 5.2 %all-to-all-start.4 = ((bf16[16,1,2,128,432]{3,4,2,1,0:T(8,128)(2,1)}), bf16[16,1,2,128,432]{3,4,2,1,0:T(8,128)(2,1)}, u32[]{:S(2)}, u32[]{:S(2)}) async-start(bf16[16,1,2,128,432]{3,4,2,1,0:T(8,128)(2,1)} %stack.29), calls=%async_computation.5 | async-start | bytes 7077888 | tf_op jit(solution)/shard_map/all_to_all | solution.py:47
  370.9 1.3 fusion.67
  372.2 6.1 %copy.142 = bf16[16,256,432]{2,1,0:T(8,128)(2,1)} copy(bf16[16,256,432]{1,2,0:T(8,128)(2,1)} %all-to-all-done.6) | data formatting | bytes 7077888 | tf_op jit(solution)/shard_map/all_to_all | solution.py:53
  378.3 1.8 slice.39
  380.1 3.0 copy.149
  383.1 2.6 multiply_reduce_fusion
  386.4 1.3 collective-permute-start.1
  388.4 22.1 %collective-permute-start.2 = (f32[]{:T(128)}, f32[]{:T(128)}, u32[]{:S(2)}, u32[]{:S(2)}) collective-permute-start(f32[]{:T(128)} %add.106), channel_id=1, source_target_pairs={{0,32},{32,0},{1,33},{33,1},{2,34},{34,2},{3,35},{35,3},{4,36},{36... | collective-permute-start | bytes 20 | tf_op jit(solution)/shard_map/ppermute | solution.py:82
  410.5 1.6 collective-permute-done.2
  412.7 1.1 collective-permute-start.3
  413.8 1.4 collective-permute-done.3
  415.8 3.1 collective-permute-start.4
  418.9 0.8 collective-permute-done.4
  420.4 4.5 copy.139
  424.9 1.6 slice.38
  426.5 1.1 copy.148
  427.6 7.8 %all-to-all-start.3 = ((bf16[128,16,320]{0,2,1:T(8,128)(2,1)}), bf16[128,16,320]{0,2,1:T(8,128)(2,1)}, u32[]{:S(2)}, u32[]{:S(2)}) async-start(bf16[128,16,320]{0,2,1:T(8,128)(2,1)} %bitcast.12), calls=%async_computation.4 | async-start | bytes 2621440 | tf_op jit(solution)/shard_map/all_to_all | solution.py:139
  435.5 5.4 %fusion.25 = f32[320,432]{1,0:T(8,128)} fusion(f32[320,432]{1,0:T(8,128)} %get-tuple-element.21, bf16[16,256,432]{1,2,0:T(8,128)(2,1)} %all-to-all-done.6, bf16[256,16,320]{0,2,1:T(8,128)(2,1)} %all-to-all-done.5), kind=kOutput, calls=%fused_computation.28 | convolution fusion | flops 1132738560 | bytes 7266304 | tf_op jit(solution)/shard_map/dot_general | solution.py:40
  440.9 1.2 reduce_sum.29
  442.2 2.9 bitcast_add_fusion.1
  445.1 1.4 fusion.63
  446.5 2.2 fusion.96
  448.7 1.7 copy.136
  450.4 0.5 copy.137
  450.9 3.2 all-to-all-done.3
  454.1 2.8 fusion.46
  456.9 2.4 fusion.41
  459.4 2.7 add_divide_fusion
  (55 shorter events, 1.0 us)
Async XLA Ops:
  7.2 192.3 %copy-start = (bf16[128,5120]{1,0:T(8,128)(2,1)S(1)}, bf16[128,5120]{1,0:T(8,128)(2,1)}, u32[]{:S(2)}) copy-start(bf16[128,5120]{1,0:T(8,128)(2,1)} %param.12) | copy-start | bytes 3932164
  11.3 7.7 %copy-start.8 = (f32[432,320]{0,1:T(8,128)S(1)}, f32[432,320]{0,1:T(8,128)}, u32[]{:S(2)}) copy-start(f32[432,320]{0,1:T(8,128)} %param.15) | copy-start | bytes 1658884
  11.3 68.5 %all-to-all-start = ((bf16[16,320,432]{2,1,0:T(8,128)(2,1)}), bf16[16,320,432]{2,1,0:T(8,128)(2,1)}, u32[]{:S(2)}, u32[]{:S(2)}) async-start(bf16[16,320,432]{2,1,0:T(8,128)(2,1)} %stack.20), calls=%async_computation | async-start | bytes 10485760 | tf_op jit(solution)/shard_map/all_to_all | solution.py:47
  82.6 66.1 %all-to-all-start.1 = ((bf16[16,320,432]{2,1,0:T(8,128)(2,1)}), bf16[16,320,432]{2,1,0:T(8,128)(2,1)}, u32[]{:S(2)}, u32[]{:S(2)}) async-start(bf16[16,320,432]{2,1,0:T(8,128)(2,1)} %stack.22), calls=%async_computation.1 | async-start | bytes 10485760 | tf_op jit(solution)/shard_map/all_to_all | solution.py:47
  87.8 2.0 copy-start.4
  87.8 108.9 %reduce-scatter.2.cloned.1.call-start = ((), (), s32[]{:S(2)}) async-start(), calls=%async_computation.8 | async-start | bytes 2949120 | tf_op jit(solution)/shard_map/reduce_scatter | solution.py:136
  89.8 2.7 copy-start.5
  92.5 4.2 copy-start.9
  148.7 4.2 slice-start
  148.7 4.2 slice-start.1
  196.8 7.6 %collective-permute-start = (bf16[32,5120]{1,0:T(8,128)(2,1)}, bf16[32,5120]{1,0:T(8,128)(2,1)S(1)}, u32[]{:S(2)}, u32[]{:S(2)}) collective-permute-start(bf16[32,5120]{1,0:T(8,128)(2,1)} %reduce-scatter.2.cloned.1.call-done), channel_id=1, source_target_pairs={{0,1},{1,0},{2,3},{3,2},{4,5},{5,4},{6,7},{7,6},{8,9},{9,8},{10,11... | collective-permute-start | bytes 983048 | tf_op jit(solution)/shard_map/ppermute | solution.py:140
  207.4 60.9 %all-to-all-start.2 = ((bf16[8,32,5120]{2,1,0:T(8,128)(2,1)}), bf16[8,32,5120]{2,1,0:T(8,128)(2,1)}, u32[]{:S(2)}, u32[]{:S(2)}) async-start(bf16[8,32,5120]{2,1,0:T(8,128)(2,1)} %stack.24), calls=%async_computation.3 | async-start | bytes 5242880 | tf_op jit(solution)/shard_map/all_to_all | solution.py:47
  270.3 55.1 %all-to-all-start.6 = ((bf16[16,256,432]{1,2,0:T(8,128)(2,1)}), bf16[16,256,432]{1,2,0:T(8,128)(2,1)}, u32[]{:S(2)}, u32[]{:S(2)}) async-start(bf16[16,256,432]{1,2,0:T(8,128)(2,1)} %broadcast_in_dim.12), calls=%async_computation.7 | async-start | bytes 7077888 | tf_op jit(solution)/shard_map/all_to_all | solution.py:53
  325.4 37.9 %all-to-all-start.5 = ((bf16[256,16,320]{0,2,1:T(8,128)(2,1)}), bf16[256,16,320]{0,2,1:T(8,128)(2,1)}, u32[]{:S(2)}, u32[]{:S(2)}) async-start(bf16[256,16,320]{0,2,1:T(8,128)(2,1)} %copy.138), calls=%async_computation.6 | async-start | bytes 5242880 | tf_op jit(solution)/shard_map/all_to_all | solution.py:147
  365.5 62.1 %all-to-all-start.4 = ((bf16[16,1,2,128,432]{3,4,2,1,0:T(8,128)(2,1)}), bf16[16,1,2,128,432]{3,4,2,1,0:T(8,128)(2,1)}, u32[]{:S(2)}, u32[]{:S(2)}) async-start(bf16[16,1,2,128,432]{3,4,2,1,0:T(8,128)(2,1)} %stack.29), calls=%async_computation.5 | async-start | bytes 7077888 | tf_op jit(solution)/shard_map/all_to_all | solution.py:47
  386.4 1.4 collective-permute-start.1
  388.4 23.7 %collective-permute-start.2 = (f32[]{:T(128)}, f32[]{:T(128)}, u32[]{:S(2)}, u32[]{:S(2)}) collective-permute-start(f32[]{:T(128)} %add.106), channel_id=1, source_target_pairs={{0,32},{32,0},{1,33},{33,1},{2,34},{34,2},{3,35},{35,3},{4,36},{36... | collective-permute-start | bytes 20 | tf_op jit(solution)/shard_map/ppermute | solution.py:82
  412.7 2.5 collective-permute-start.3
  415.8 4.0 collective-permute-start.4
  427.6 26.5 %all-to-all-start.3 = ((bf16[128,16,320]{0,2,1:T(8,128)(2,1)}), bf16[128,16,320]{0,2,1:T(8,128)(2,1)}, u32[]{:S(2)}, u32[]{:S(2)}) async-start(bf16[128,16,320]{0,2,1:T(8,128)(2,1)} %bitcast.12), calls=%async_computation.4 | async-start | bytes 2621440 | tf_op jit(solution)/shard_map/all_to_all | solution.py:139
  435.5 6.7 %copy-start.2 = (bf16[128,1,16,432]{0,3,2,1:T(8,128)(2,1)S(1)}, bf16[128,1,16,432]{0,3,2,1:T(8,128)(2,1)}, u32[]{:S(2)}) copy-start(bf16[128,1,16,432]{0,3,2,1:T(8,128)(2,1)} %copy.149) | copy-start | bytes 5308420
  442.1 2.9 copy-start.3
  442.1 2.9 copy-start.6
  450.4 3.7 copy-start.10
  454.1 2.8 copy-start.7
  456.9 2.5 copy-start.12
  456.9 2.5 copy-start.11
  459.4 2.8 copy-start.1
Sparse Core Ops, SparseCore 0:
  156.2 40.5 reduce-scatter.1
